TPU v7x, 16 devices: a 4x2x1 block of a 4x4x8 slice. The times are simulated.
16 devices in a mesh: dp: 4 (over y, z, core), sp: 4 (over x).
Axes of the slice: x: 4, y: 2, z: 1, core: 2. Of those that a mesh axis runs over, the one named last changes fastest.
The devices are a block of a 4x4x8 slice.
Arguments:
- q: bfloat16 [128, 48, 256], P('dp'), parts along dimension 0
- k: bfloat16 [128, 8192, 1, 256], P('dp', 'sp'), parts along dimension 0
- v: bfloat16 [128, 8192, 1, 256], P('dp', 'sp'), parts along dimension 0
Outputs:
- q: bfloat16 [128, 48, 256], P('dp'), parts along dimension 0
There are 4 independent parts. A program takes and returns all parts, laid end to end along the dimension named above; each array names one.
All inputs are finite; a program needn't handle non-finite values.
Results may differ from a plain program's by a relative error of at most 0.012.
Values are sent between devices in bfloat16 or wider.
A program may use at most 768 MiB of HBM per device.

v0:
```python
import jax
import jax.numpy as jnp
from jax import lax
from jax.sharding import PartitionSpec as P


def einsum(form, a, b):
    return jnp.einsum(form, a.astype(jnp.float32), b.astype(jnp.float32))


def part_of(q, k, v):
    grouped = q.reshape(q.shape[0], k.shape[2], -1, q.shape[2])
    scores = einsum("bgsd,bugd->bgsu", grouped, k) * q.shape[2] ** -0.5
    high = jnp.max(scores, -1, keepdims=True)
    weights = jnp.exp(scores - high)
    seen = einsum("bgsu,bugd->bgsd", weights.astype(jnp.bfloat16), v)
    return jnp.concatenate([seen, jnp.sum(weights, -1, keepdims=True), high], -1)


def together(parts):
    seen, total, high = parts[..., :-2], parts[..., -2:-1], parts[..., -1:]
    scale = jnp.exp(high - jnp.max(high, 0))
    return (jnp.sum(seen * scale, 0) / jnp.sum(total * scale, 0)).astype(jnp.bfloat16)


def solution(mesh):
    def step(q, k, v):
        return together(lax.all_gather(part_of(q, k, v), "sp")).reshape(q.shape)

    return jax.shard_map(
        step,
        mesh=mesh,
        in_specs=(P("dp", None, None), P("dp", "sp", None, None), P("dp", "sp", None, None)),
        out_specs=P("dp", None, None),
        check_vma=False,
    )
```

profile of v0, /device:TPU:112, one launch (start us, length us, event | category | flops | bytes accessed | tf_op | source)
XLA Modules:
  0.0 191.3 jit_solution(11097753602074645690)
XLA Ops:
  6.5 0.0 copy-start
  6.6 0.0 all-gather.3.cloned.1.call-start
  6.6 1.1 copy-done
  7.7 20.5 %multiply_reduce_fusion = (f32[32,48]{1,0:T(8,128)S(1)}, f32[32,48,2048]{2,1,0:T(8,128)}) fusion(bf16[32,48,256]{2,1,0:T(8,128)(2,1)S(1)} %copy-done, bf16[32,2048,1,256]{3,1,2,0:T(8,128)(2,1)} %param.4), kind=kOutput, calls=%fused_computation.7 | convolution fusion | flops 1616902656 | bytes 46929920 | tf_op jit(solution)/shard_map/bgsd,bugd->bgsu/dot_general | solution.py:8
  28.2 6.8 %fusion.5 = f32[32,48]{1,0:T(8,128)S(1)} fusion(f32[32,48,2048]{2,1,0:T(8,128)} %get-tuple-element.8, f32[32,48]{1,0:T(8,128)S(1)} %get-tuple-element.7), kind=kLoop, calls=%fused_computation.8 | loop fusion | flops 9435648 | bytes 12595200 | tf_op jit(solution)/shard_map/reduce_sum | solution.py:17
  35.0 17.0 %fusion.10 = f32[32,1,48,256]{3,2,0,1:T(8,128)S(1)} fusion(bf16[32,2048,1,256]{3,1,2,0:T(8,128)(2,1)} %param.5, f32[32,48,2048]{2,1,0:T(8,128)} %get-tuple-element.8, f32[32,48]{1,0:T(8,128)S(1)} %get-tuple-element.7), kind=kOutput, calls=%fused_computation.14 | convolution fusion | flops 1620049920 | bytes 47716352 | tf_op jit(solution)/shard_map/bgsu,bugd->bgsd/dot_general | solution.py:8
  52.0 0.3 copy.12
  52.3 0.3 copy.13
  52.7 1.7 maximum_bitcast_fusion
  54.4 0.1 all-gather.3.cloned.1.call-update
  54.5 91.2 %all-gather.3.cloned.1.call-done = f32[128,1,48,258]{3,2,1,0:T(8,128)} async-done(((f32[32,1,48,258]{3,2,1,0:T(8,128)}), f32[128,1,48,258]{3,2,1,0:T(8,128)}) %all-gather.3.cloned.1.call-update) | async-done | bytes 6340624 | tf_op jit(solution)/shard_map/all_gather | solution.py:28
  145.7 21.0 %copy.15 = f32[128,1,48,258]{2,0,3,1:T(8,128)} copy(f32[128,1,48,258]{3,2,1,0:T(8,128)} %all-gather.3.cloned.1.call-done) | data formatting | bytes 12681216 | tf_op jit(solution)/shard_map/all_gather | solution.py:28
  166.6 0.9 slice_reduce_fusion
  167.5 0.9 fusion.15
  168.4 0.0 copy-start.1
  168.4 10.9 %fusion.4 = f32[32,48,256]{1,0,2:T(8,128)} fusion(f32[4,32,1,48,258]{3,1,0,4,2:T(8,128)} %bitcast.22, f32[4,32,48]{2,1,0:T(8,128)S(1)} %get-tuple-element.6), kind=kLoop, calls=%fused_computation.5 | loop fusion | flops 2752512 | bytes 7888896 | tf_op jit(solution)/shard_map/reduce_sum | solution.py:23
  179.4 2.7 %divide_convert_fusion = bf16[32,48,256]{1,0,2:T(8,128)(2,1)S(1)} fusion(f32[32,48,256]{1,0,2:T(8,128)} %fusion.4, f32[32,48]{1,0:T(8,128)S(1)} %get-tuple-element.5), kind=kLoop, calls=%fused_computation.12 | loop fusion | flops 786432 | bytes 2365440 | tf_op jit(solution)/shard_map/convert_element_type | solution.py:23
  182.1 2.4 %copy.16 = bf16[32,48,256]{2,1,0:T(8,128)(2,1)} copy(bf16[32,48,256]{1,0,2:T(8,128)(2,1)S(1)} %divide_convert_fusion) | data formatting | bytes 1572864 | tf_op jit(solution)/shard_map/convert_element_type | solution.py:23
  184.5 0.0 copy-done.1
Async XLA Ops:
  6.5 1.1 copy-start
  6.6 139.1 %all-gather.3.cloned.1.call-start = ((), (), s32[]{:S(2)}) async-start(), calls=%async_computation | async-start | bytes 11796480 | tf_op jit(solution)/shard_map/all_gather | solution.py:28
  168.4 16.1 %copy-start.1 = (bf16[32,48,256]{2,1,0:T(8,128)(2,1)S(1)}, bf16[32,48,256]{2,1,0:T(8,128)(2,1)}, u32[]{:S(2)}) copy-start(bf16[32,48,256]{2,1,0:T(8,128)(2,1)} %param.3) | copy-start | bytes 2359300
Sparse Core Ops, SparseCore 0:
  54.6 91.0 all-gather.2
where the time goes:
time: 192 us; the launch traced here: 191 us
  waiting for transfers between devices  91.3 us (48%)
  matrix products  37.5 us (20%)
  local copies, waits for them, and re-layouts  25.2 us (13%)
  other arithmetic  23.9 us (12%)
  between operations  13.5 us (7%)
    all_gather x1, waiting for transfers between devices, step(): return together(lax.all_gather(part_of(q, k, v), 'sp')).reshape(q.shape)  91.2 us
    dot_general x2, matrix products, einsum(): return jnp.einsum(form, a.astype(jnp.float32), b.astype(jnp.float32))  37.5 us
    all_gather x1, local copies, waits for them, and re-layouts, step(): return together(lax.all_gather(part_of(q, k, v), 'sp')).reshape(q.shape)  21 us
    reduce_sum x1, other arithmetic, together(): jnp.sum(seen * scale, 0) / jnp.sum(total * scale, 0)  10.9 us
    reduce_sum x1, other arithmetic, part_of(): jnp.sum(weights, -1, keepdims=True)  6.78 us
  transfers between devices with their start and end apart: 1, of which 1 were waited for; matrix products, arithmetic and copies ran while one was open for 0% of the time, Pallas kernels for 0%

commit v1 on v0

v1 whole, which is shorter than its diff:
```python
import functools
import math

import jax
import jax.numpy as jnp
from jax import lax
from jax.experimental import pallas as pl
from jax.experimental.pallas import tpu as pltpu
from jax.sharding import PartitionSpec as P

MESH = pl.DeviceIdType.MESH
F32, BF16 = jnp.float32, jnp.bfloat16
SLOTS = 8
RUN = 256


def kernel(n, scale, q_hbm, k_hbm, v_hbm, out, qbuf, kbuf, vbuf, score, top, own, part, stat, got, got_stat, qsem, ksem, vsem, psend, precv, ssend, srecv, asend, arecv):
    count, heads, head = q_hbm.shape
    keys = k_hbm.shape[1]
    groups = count // n
    runs = keys // RUN
    me, dp = lax.axis_index("sp"), lax.axis_index("dp")
    peer = [lax.rem(me + o, n) for o in range(n)]

    def k_copy(i, slot):
        return pltpu.make_async_copy(k_hbm.at[i], kbuf.at[slot], ksem.at[slot])

    def v_copy(i, slot):
        return pltpu.make_async_copy(v_hbm.at[i], vbuf.at[slot], vsem.at[slot])

    q_copy = pltpu.make_async_copy(q_hbm, qbuf, qsem)
    k_copy(0, 0).start(priority=1)
    q_copy.start(priority=1)
    v_copy(0, 0).start(priority=1)
    for i in range(1, SLOTS):
        k_copy(i, i).start(priority=1)
        v_copy(i, i).start(priority=1)
    barrier = pltpu.get_barrier_semaphore()
    for o in range(1, n):
        pl.semaphore_signal(barrier, inc=1, device_id=(dp, peer[o]), device_id_type=MESH)

    rows = lax.broadcasted_iota(jnp.int32, (heads, 128), 0)
    lanes = lax.broadcasted_iota(jnp.int32, (heads, 128), 1)
    diagonal = rows == lanes

    def as_row(column):
        return jnp.sum(jnp.where(diagonal, column, 0.0), 0, keepdims=True)

    def as_column(row):
        return jnp.sum(jnp.where(diagonal, row, 0.0), 1, keepdims=True)

    def both(a, a_slot, a_par, b, b_slot, b_par):
        if b is not None:
            high = jnp.max(top[b_par], 1, keepdims=True)
            total = jnp.zeros((heads, 128), F32)
            seen = jnp.zeros((heads, head), F32)
        largest = None
        if a is not None:
            q = qbuf[a]
        for r in range(runs):
            at = pl.ds(r * RUN, RUN)
            if a is not None:
                s = lax.dot_general(q, kbuf[a_slot, at, :], (((1,), (1,)), ((), ())), preferred_element_type=F32)
                score[a_par, :, at] = s
                m = functools.reduce(jnp.maximum, [s[:, c : c + 128] for c in range(0, RUN, 128)])
                largest = m if largest is None else jnp.maximum(largest, m)
            if b is not None:
                w = jnp.exp2((score[b_par, :, at] - high) * scale)
                for c in range(0, RUN, 128):
                    total += w[:, c : c + 128]
                seen += jnp.dot(w.astype(BF16), vbuf[b_slot, at, :], preferred_element_type=F32)
        if a is not None:
            top[a_par] = largest
        if b is not None:
            own[b] = seen
            part[b] = seen.astype(BF16)
            stat[b, 0:1] = as_row(high)
            stat[b, 1:2] = as_row(jnp.sum(total, 1, keepdims=True))

    def part_copies(g, o):
        i = g * n + peer[o]
        to = (dp, peer[o])
        return (
            pltpu.make_async_remote_copy(part.at[i], got.at[g, o - 1], psend.at[g, o - 1], precv.at[g, o - 1], device_id=to, device_id_type=MESH),
            pltpu.make_async_remote_copy(stat.at[i], got_stat.at[g, o - 1], ssend.at[g, o - 1], srecv.at[g, o - 1], device_id=to, device_id_type=MESH),
        )

    def result_copy(g, o):
        i = g * n + me
        return pltpu.make_async_remote_copy(out.at[i], out.at[i], asend.at[g, o - 1], arecv.at[g, o - 1], device_id=(dp, peer[o]), device_id_type=MESH)

    def send_parts(g):
        for o in range(1, n):
            for copy in part_copies(g, o):
                copy.start()

    def combine(i, parts, stats):
        highs, totals = [s[0:1] for s in stats], [s[1:2] for s in stats]
        most = functools.reduce(jnp.maximum, highs)
        ws = [jnp.exp2((h - most) * scale) for h in highs]
        whole = sum(t * w for t, w in zip(totals, ws))
        out[i] = sum(p.astype(F32) * as_column(w / whole) for p, w in zip(parts, ws)).astype(BF16)

    def finish(g):
        i = g * n + me
        for o in range(1, n):
            for copy in part_copies(g, o):
                copy.wait_recv()
        combine(i, [own[i]] + [got[g, o] for o in range(n - 1)], [stat[i]] + [got_stat[g, o] for o in range(n - 1)])
        for o in range(1, n):
            result_copy(g, o).start()

    def advance(i, slot, next_slot, par, last=False):
        if not last:
            k_copy(i + 1, next_slot).wait()
        v_copy(i, slot).wait()
        both(None if last else i + 1, next_slot, 1 - par, i, slot, par)

    q_copy.wait()
    k_copy(0, 0).wait()
    both(0, 0, 0, None, None, None)
    k_copy(SLOTS, 0).start(priority=1)

    def group(g, carry):
        for j in range(n):
            i = g * n + j
            slot, next_slot = lax.rem(i, SLOTS), lax.rem(i + 1, SLOTS)
            advance(i, slot, next_slot, j % 2)

            @pl.when(i + 1 + SLOTS < count)
            def _():
                k_copy(i + 1 + SLOTS, next_slot).start(priority=1)

            @pl.when(i + SLOTS < count)
            def _():
                v_copy(i + SLOTS, slot).start(priority=1)

        @pl.when(g == 0)
        def _():
            pl.semaphore_wait(barrier, n - 1)

        send_parts(g)

        @pl.when(g > 0)
        def _():
            finish(g - 1)

        return carry

    last = groups - 1
    lax.fori_loop(0, last, group, 0)

    def tail_copies(j, o):
        i = last * n + j
        to = (dp, peer[o])
        at = last + j
        return (
            pltpu.make_async_remote_copy(part.at[i], got.at[at, o - 1], psend.at[at, o - 1], precv.at[at, o - 1], device_id=to, device_id_type=MESH),
            pltpu.make_async_remote_copy(stat.at[i], got_stat.at[at, o - 1], ssend.at[at, o - 1], srecv.at[at, o - 1], device_id=to, device_id_type=MESH),
        )

    for j in range(n):
        i = last * n + j
        advance(i, i % SLOTS, (i + 1) % SLOTS, j % 2, last=j == n - 1)
        for o in range(1, n):
            for copy in tail_copies(j, o):
                copy.start()
        if j == 0:
            finish(last - 1)
    for j in range(n):
        i = last * n + j
        at = last + j
        for o in range(1, n):
            for copy in tail_copies(j, o):
                copy.wait_recv()
        combine(i, [own[i]] + [got[at, o] for o in range(n - 1)], [stat[i]] + [got_stat[at, o] for o in range(n - 1)])

    def drain(g, carry):
        for o in range(1, n):
            for copy in part_copies(g, o):
                copy.wait_send()
            result_copy(g, o).wait()
        return carry

    lax.fori_loop(0, last, drain, 0)
    for j in range(n):
        for o in range(1, n):
            for copy in tail_copies(j, o):
                copy.wait_send()


def attend(n, q, k, v):
    count, heads, head = q.shape
    keys = k.shape[1]
    q = pltpu.with_memory_space_constraint(q, pltpu.HBM)
    k, v = k.reshape(count, keys, head), v.reshape(count, keys, head)
    scale = head**-0.5 * math.log2(math.e)
    groups = count // n
    slots = groups - 1 + n
    dma = pltpu.SemaphoreType.DMA
    return pl.pallas_call(
        functools.partial(kernel, n, scale),
        out_shape=jax.ShapeDtypeStruct(q.shape, q.dtype),
        in_specs=[pl.BlockSpec(memory_space=pltpu.HBM)] * 3,
        out_specs=pl.BlockSpec(memory_space=pltpu.VMEM),
        scratch_shapes=[
            pltpu.VMEM((count, heads, head), BF16),
            pltpu.VMEM((SLOTS, keys, head), BF16),
            pltpu.VMEM((SLOTS, keys, head), BF16),
            pltpu.VMEM((2, heads, keys), F32),
            pltpu.VMEM((2, heads, 128), F32),
            pltpu.VMEM((count, heads, head), F32),
            pltpu.VMEM((count, heads, head), BF16),
            pltpu.VMEM((count, 2, 128), F32),
            pltpu.VMEM((slots, n - 1, heads, head), BF16),
            pltpu.VMEM((slots, n - 1, 2, 128), F32),
            dma,
            dma((SLOTS,)),
            dma((SLOTS,)),
            dma((slots, n - 1)),
            dma((slots, n - 1)),
            dma((slots, n - 1)),
            dma((slots, n - 1)),
            dma((groups - 1, n - 1)),
            dma((groups - 1, n - 1)),
        ],
        compiler_params=pltpu.CompilerParams(collective_id=0, has_side_effects=True, vmem_limit_bytes=52 * 2**20),
    )(q, k, v)


def solution(mesh):
    return jax.shard_map(
        functools.partial(attend, mesh.shape["sp"]),
        mesh=mesh,
        in_specs=(P("dp", None, None), P("dp", "sp", None, None), P("dp", "sp", None, None)),
        out_specs=P("dp", None, None),
        check_vma=False,
    )
```

time: 192 us -> 43 us (0.22)
  waiting for transfers between devices: 91.3 us -> 0 us
  Pallas kernels: 0 us -> 42 us
  matrix products: 37.5 us -> 0 us
  local copies, waits for them, and re-layouts: 25.2 us -> 0.88 us
  other arithmetic: 23.9 us -> 0 us
  between operations: 13.5 us -> 0.01 us
    all_gather x1 -> x0, waiting for transfers between devices: 91.2 us -> none  [step(): return together(lax.all_gather(part_of(q, k, v), 'sp')).reshape(q.shape)]
    pallas_call x0 -> x1, Pallas kernels: none -> 42 us  [attend(): pl.pallas_call(functools.partial(kernel, n, scale), out_shape=jax.ShapeDt...]
    dot_general x2 -> x0, matrix products: 37.5 us -> none  [einsum(): return jnp.einsum(form, a.astype(jnp.float32), b.astype(jnp.float32))]
    all_gather x1 -> x0, local copies, waits for them, and re-layouts: 21 us -> none  [step(): return together(lax.all_gather(part_of(q, k, v), 'sp')).reshape(q.shape)]
    reduce_sum x3 -> x0, other arithmetic: 18.6 us -> none  [the longest x1 10.9 us: together(): jnp.sum(seen * scale, 0) / jnp.sum(total * scale, 0)]
    convert_element_type x1 -> x0, other arithmetic: 2.7 us -> none  [together(): (jnp.sum(seen * scale, 0) / jnp.sum(total * scale, 0)).astype(jnp.bfloat16)]
    convert_element_type x1 -> x0, local copies, waits for them, and re-layouts: 2.43 us -> none  [together(): (jnp.sum(seen * scale, 0) / jnp.sum(total * scale, 0)).astype(jnp.bfloat16)]
  transfers between devices with their start and end apart: 1 -> 0, of which waited for: 1 -> 0; matrix products, arithmetic and copies ran while one was open for 0% -> 0% of each run, Pallas kernels for 0% -> 0%
where the time goes in v1:
time: 43 us; the launch traced here: 42.9 us
  Pallas kernels  42 us (98%)
  local copies, waits for them, and re-layouts  0.88 us (2%)
    pallas_call x1, Pallas kernels, attend(): pl.pallas_call(functools.partial(kernel, n, scale), out_shape=jax.ShapeDt...  42 us
    unnamed x1, local copies, waits for them, and re-layouts  0.88 us

profile of v1, /device:TPU:112, one launch (start us, length us, event | category | flops | bytes accessed | tf_op | source)
XLA Modules:
  0.0 42.9 jit_solution(10920777437365319144)
XLA Ops:
  0.0 42.0 %shard_map.37 = bf16[32,48,256]{2,1,0:T(8,128)(2,1)S(1)} custom-call(bf16[32,48,256]{2,1,0:T(8,128)(2,1)} %q_hbm.1, bf16[32,2048,256]{2,1,0:T(8,128)(2,1)} %bitcast.2, bf16[32,2048,256]{2,1,0:T(8,128)(2,1)} %bitcast.3), custom_call_target="tpu_custom_call" | custom-call | tf_op jit(solution)/shard_map/pallas_call | solution.py:201
  42.0 0.9 %copy.5 = bf16[32,48,256]{2,1,0:T(8,128)(2,1)} copy(bf16[32,48,256]{2,1,0:T(8,128)(2,1)S(1)} %shard_map.37) | data formatting | bytes 1572864

commit v2 on v0

v2 whole, which is shorter than its diff:
```python
import functools
import math

import jax
import jax.numpy as jnp
from jax import lax
from jax.experimental import pallas as pl
from jax.experimental.pallas import tpu as pltpu
from jax.sharding import PartitionSpec as P

MESH = pl.DeviceIdType.MESH
F32, BF16 = jnp.float32, jnp.bfloat16
SLOTS = 8
DEPTH = 4
RUN = 256
GAP = 11
LATE = 4
HEAD, BLOCK, TAIL = 0, 2, 4


def plan(groups, n):
    away = [n // 2] + [o for o in range(1, n) if o != n // 2]
    others = [(g, o) for g in range(groups) for o in away]
    order, used = [], 0
    for g in range(groups):
        until = len(others) if g >= groups - LATE else min(g * (n - 1) + GAP, len(others))
        order += others[used:until] + [(g, 0)]
        used = until
    return order


def split(steps):
    sizes = [1] * HEAD + [BLOCK] * ((steps - HEAD - TAIL) // BLOCK)
    sizes += [1] * (steps - sum(sizes))
    ends = [sum(sizes[: i + 1]) for i in range(len(sizes))]
    return [list(range(e - z, e)) for e, z in zip(ends, sizes)]


def kernel(n, scale, q_hbm, k_hbm, v_hbm, out, qbuf, kbuf, vbuf, score, top, part, stat, got, got_stat, qsem, ksem, vsem, psend, precv, ssend, srecv, asend, arecv):
    count, heads, head = q_hbm.shape
    keys = k_hbm.shape[1]
    groups = count // n
    me, dp = lax.axis_index("sp"), lax.axis_index("dp")
    peer = [lax.rem(me + o, n) for o in range(n)]
    order = plan(groups, n)
    seq = [g * n + peer[o] for g, o in order]

    def k_copy(t):
        return pltpu.make_async_copy(k_hbm.at[seq[t]], kbuf.at[t % SLOTS], ksem.at[t % SLOTS])

    def v_copy(t):
        return pltpu.make_async_copy(v_hbm.at[seq[t]], vbuf.at[t % SLOTS], vsem.at[t % SLOTS])

    q_copy = pltpu.make_async_copy(q_hbm, qbuf, qsem)
    k_copy(0).start(priority=0)
    q_copy.start(priority=0)
    k_copy(1).start(priority=0)
    v_copy(0).start(priority=1)
    v_copy(1).start(priority=1)
    for t in range(2, SLOTS):
        k_copy(t).start(priority=1)
        v_copy(t).start(priority=1)
    barrier = pltpu.get_barrier_semaphore()
    for o in range(1, n):
        pl.semaphore_signal(barrier, inc=1, device_id=(dp, peer[o]), device_id_type=MESH)

    rows = lax.broadcasted_iota(jnp.int32, (heads, heads), 0)
    lanes = lax.broadcasted_iota(jnp.int32, (heads, heads), 1)
    diagonal = rows == lanes

    def as_column(row):
        return jnp.sum(jnp.where(diagonal, row, 0.0), 1, keepdims=True)

    def attend(ahead, now):
        largest = {}
        high = {b: jnp.max(top[b % DEPTH], 0, keepdims=True) for b in now}
        total = {b: jnp.zeros((8, heads), F32) for b in now}
        seen = {b: jnp.zeros((heads, head), F32) for b in now}
        for r in range(keys // RUN):
            at = pl.ds(r * RUN, RUN)
            for a in ahead:
                s = lax.dot_general(kbuf[a % SLOTS, at, :], qbuf[seq[a]], (((1,), (1,)), ((), ())), preferred_element_type=F32)
                score[a % DEPTH, at, :] = s
                m = jnp.max(s.reshape(RUN // 8, 8, heads), 0)
                largest[a] = m if r == 0 else jnp.maximum(largest[a], m)
            for b in now:
                w = jnp.exp2((score[b % DEPTH, at, :] - high[b]) * scale)
                total[b] += jnp.sum(w.reshape(RUN // 8, 8, heads), 0)
                seen[b] += lax.dot_general(w.astype(BF16), vbuf[b % SLOTS, at, :], (((0,), (0,)), ((), ())), preferred_element_type=F32)
        for a in ahead:
            top[a % DEPTH] = largest[a]
        return [(seen[b], high[b], jnp.sum(total[b], 0, keepdims=True)) for b in now]

    def part_copies(g, o):
        to = (dp, peer[o])
        return (
            pltpu.make_async_remote_copy(part.at[g, o - 1], got.at[g, o - 1], psend.at[g, o - 1], precv.at[g, o - 1], device_id=to, device_id_type=MESH),
            pltpu.make_async_remote_copy(stat.at[g, o - 1], got_stat.at[g, o - 1], ssend.at[g, o - 1], srecv.at[g, o - 1], device_id=to, device_id_type=MESH),
        )

    def result_copy(g, o):
        i = g * n + me
        return pltpu.make_async_remote_copy(out.at[i], out.at[i], asend.at[g, o - 1], arecv.at[g, o - 1], device_id=(dp, peer[o]), device_id_type=MESH)

    def finish(g, seen, high, total):
        i = g * n + me
        for o in range(1, n):
            for copy in part_copies(g, o):
                copy.wait_recv()
        parts = [seen] + [got[g, o] for o in range(n - 1)]
        highs = [high] + [got_stat[g, o, 0:1] for o in range(n - 1)]
        totals = [total] + [got_stat[g, o, 1:2] for o in range(n - 1)]
        most = functools.reduce(jnp.maximum, highs)
        ws = [jnp.exp2((h - most) * scale) for h in highs]
        whole = sum(t * w for t, w in zip(totals, ws))
        out[i] = sum(p.astype(F32) * as_column(w / whole) for p, w in zip(parts, ws)).astype(BF16)
        pending.extend(result_copy(g, o) for o in (2, 1, 3))
        if g >= groups - LATE - 1:
            while pending:
                pending.pop(0).start()

    steps = len(order)
    blocks = split(steps)
    pending = []
    q_copy.wait()
    for t in blocks[0]:
        k_copy(t).wait()
    attend(blocks[0], [])
    for i, now in enumerate(blocks):
        ahead = blocks[i + 1] if i + 1 < len(blocks) else []
        for t in now:
            if t + SLOTS < steps:
                k_copy(t + SLOTS).start(priority=1)
        for t in ahead:
            k_copy(t).wait()
        for t in now:
            v_copy(t).wait()
        found = attend(ahead, now)
        for t, (seen, high, total) in zip(now, found):
            g, o = order[t]
            if t + SLOTS < steps:
                v_copy(t + SLOTS).start(priority=1)
            if o:
                part[g, o - 1] = seen.astype(BF16)
                stat[g, o - 1, 0:1] = high
                stat[g, o - 1, 1:2] = total
                if t == 0:
                    pl.semaphore_wait(barrier, n - 1)
                for copy in part_copies(g, o):
                    copy.start()
                if pending:
                    pending.pop(0).start()
            else:
                finish(g, seen, high, total)

    def drain(g, carry):
        for o in range(1, n):
            for copy in part_copies(g, o):
                copy.wait_send()
            result_copy(g, o).wait()
        return carry

    lax.fori_loop(0, groups, drain, 0)


def attention(n, q, k, v):
    count, heads, head = q.shape
    keys = k.shape[1]
    q = pltpu.with_memory_space_constraint(q, pltpu.HBM)
    k, v = k.reshape(count, keys, head), v.reshape(count, keys, head)
    scale = head**-0.5 * math.log2(math.e)
    groups = count // n
    dma = pltpu.SemaphoreType.DMA
    return pl.pallas_call(
        functools.partial(kernel, n, scale),
        out_shape=jax.ShapeDtypeStruct(q.shape, q.dtype),
        in_specs=[pl.BlockSpec(memory_space=pltpu.HBM)] * 3,
        out_specs=pl.BlockSpec(memory_space=pltpu.VMEM),
        scratch_shapes=[
            pltpu.VMEM((count, heads, head), BF16),
            pltpu.VMEM((SLOTS, keys, head), BF16),
            pltpu.VMEM((SLOTS, keys, head), BF16),
            pltpu.VMEM((DEPTH, keys, heads), F32),
            pltpu.VMEM((DEPTH, 8, heads), F32),
            pltpu.VMEM((groups, n - 1, heads, head), BF16),
            pltpu.VMEM((groups, n - 1, 2, heads), F32),
            pltpu.VMEM((groups, n - 1, heads, head), BF16),
            pltpu.VMEM((groups, n - 1, 2, heads), F32),
            dma,
            dma((SLOTS,)),
            dma((SLOTS,)),
        ]
        + [dma((groups, n - 1))] * 6,
        compiler_params=pltpu.CompilerParams(collective_id=0, has_side_effects=True, vmem_limit_bytes=52 * 2**20),
    )(q, k, v)


def solution(mesh):
    return jax.shard_map(
        functools.partial(attention, mesh.shape["sp"]),
        mesh=mesh,
        in_specs=(P("dp", None, None), P("dp", "sp", None, None), P("dp", "sp", None, None)),
        out_specs=P("dp", None, None),
        check_vma=False,
    )
```

time: 192 us -> 31.8 us (0.17)
  waiting for transfers between devices: 91.3 us -> 0 us
  matrix products: 37.5 us -> 0 us
  Pallas kernels: 0 us -> 30.9 us
  local copies, waits for them, and re-layouts: 25.2 us -> 0.88 us
  other arithmetic: 23.9 us -> 0 us
  between operations: 13.5 us -> 0.01 us
    all_gather x1 -> x0, waiting for transfers between devices: 91.2 us -> none  [step(): return together(lax.all_gather(part_of(q, k, v), 'sp')).reshape(q.shape)]
    dot_general x2 -> x0, matrix products: 37.5 us -> none  [einsum(): return jnp.einsum(form, a.astype(jnp.float32), b.astype(jnp.float32))]
    pallas_call x0 -> x1, Pallas kernels: none -> 30.9 us  [attention(): pl.pallas_call(functools.partial(kernel, n, scale), out_shape=jax.ShapeDt...]
    all_gather x1 -> x0, local copies, waits for them, and re-layouts: 21 us -> none  [step(): return together(lax.all_gather(part_of(q, k, v), 'sp')).reshape(q.shape)]
    reduce_sum x3 -> x0, other arithmetic: 18.6 us -> none  [the longest x1 10.9 us: together(): jnp.sum(seen * scale, 0) / jnp.sum(total * scale, 0)]
    convert_element_type x1 -> x0, other arithmetic: 2.7 us -> none  [together(): (jnp.sum(seen * scale, 0) / jnp.sum(total * scale, 0)).astype(jnp.bfloat16)]
    convert_element_type x1 -> x0, local copies, waits for them, and re-layouts: 2.43 us -> none  [together(): (jnp.sum(seen * scale, 0) / jnp.sum(total * scale, 0)).astype(jnp.bfloat16)]
  transfers between devices with their start and end apart: 1 -> 0, of which waited for: 1 -> 0; matrix products, arithmetic and copies ran while one was open for 0% -> 0% of each run, Pallas kernels for 0% -> 0%
where the time goes in v2:
time: 31.8 us
  Pallas kernels  30.9 us (97%)
  local copies, waits for them, and re-layouts  0.88 us (3%)
    pallas_call x1, Pallas kernels, attention(): pl.pallas_call(functools.partial(kernel, n, scale), out_shape=jax.ShapeDt...  30.9 us
    unnamed x1, local copies, waits for them, and re-layouts  0.88 us

profile of v2, /device:TPU:112, one launch (start us, length us, event | category | flops | bytes accessed | tf_op | source)
XLA Modules:
  0.0 31.8 jit_solution(3497592079267585970)
XLA Ops:
  0.0 30.9 %shard_map.37 = bf16[32,48,256]{2,1,0:T(8,128)(2,1)S(1)} custom-call(bf16[32,48,256]{2,1,0:T(8,128)(2,1)} %q_hbm.1, bf16[32,2048,256]{2,1,0:T(8,128)(2,1)} %bitcast.2, bf16[32,2048,256]{2,1,0:T(8,128)(2,1)} %bitcast.3), custom_call_target="tpu_custom_call" | custom-call | tf_op jit(solution)/shard_map/pallas_call | solution.py:174
  30.9 0.9 %copy.5 = bf16[32,48,256]{2,1,0:T(8,128)(2,1)} copy(bf16[32,48,256]{2,1,0:T(8,128)(2,1)S(1)} %shard_map.37) | data formatting | bytes 1572864
